TPU v7x, 32 devices: a whole 2x2x4 slice. The times are simulated.
32 devices in a mesh: dp: 8 (over z, x), col: 4 (over y, core).
Axes of the slice: x: 2, y: 2, z: 4, core: 2. Of those that a mesh axis runs over, the one named last changes fastest.
Arguments:
- tokens: bfloat16 [50432, 384], P(('dp', 'col')), may hold values from -40 to 40
- packed: bfloat16 [384, 1152], P('dp', 'col'), may hold values from -0.3125 to 0.3125
- packed_bias: float32 [1152], P('col'), may hold values from -3 to 3
- projection: bfloat16 [384, 384], P('col', 'dp'), may hold values from -2.5 to 2.5
- projection_bias: float32 [384], replicated, may hold values from -3 to 3
- expansion: bfloat16 [384, 1536], P('dp', 'col'), may hold values from -0.3125 to 0.3125
- expansion_bias: float32 [1536], P('col'), may hold values from -3 to 3
- reduction: bfloat16 [1536, 384], P('col', 'dp'), may hold values from -0.15625 to 0.15625
- reduction_bias: float32 [384], replicated, may hold values from -3 to 3
- first_scale: float32 [384], replicated, may hold values from 0.25 to 1.75
- first_shift: float32 [384], replicated, may hold values from -3 to 3
- second_scale: float32 [384], replicated, may hold values from 0.25 to 1.75
- second_shift: float32 [384], replicated, may hold values from -3 to 3
- upstream: bfloat16 [50432, 384], P(('dp', 'col')), may hold values from -6 to 6
Outputs:
- layer_output: bfloat16 [50432, 384], P(('dp', 'col'))
- input_grad: float32 [50432, 384], P(('dp', 'col'))
- packed_grad: float32 [384, 1152], P('dp', 'col')
- projection_grad: float32 [384, 384], P('col', 'dp')
- expansion_grad: float32 [384, 1536], P('dp', 'col')
- reduction_grad: float32 [1536, 384], P('col', 'dp')
- packed_bias_grad: float32 [1152], P('col')
- projection_bias_grad: float32 [384], P('col')
- expansion_bias_grad: float32 [1536], P('col')
- reduction_bias_grad: float32 [384], P('col')
- first_scale_grad: float32 [384], P('col')
- first_shift_grad: float32 [384], P('col')
- second_scale_grad: float32 [384], P('col')
- second_shift_grad: float32 [384], P('col')
All inputs are finite; a program needn't handle non-finite values.
Results may differ from a plain program's by a relative error of at most 0.023.
Values may be sent and summed in bfloat16 or wider, within the bound.
A program may use at most 192 MiB of HBM per device.

v0:
```python
import jax
import jax.numpy as jnp
from jax import lax
from jax.sharding import PartitionSpec as P

D = 384
HEADS = 6
SEQ = 197
epsilon = 1e-06
root_half = 0.7071067811865476
inv_root_tau = 0.3989422804014327


def gelu_slope(values):
    return (
        0.5 * (1.0 + lax.erf(values * root_half))
        + values * jnp.exp(-0.5 * values * values) * inv_root_tau
    )


def contract_rows(left, right):
    return lax.dot_general(
        left, right, (((0,), (0,)), ((), ())), preferred_element_type=jnp.float32
    )


def contract_cols(left, right):
    return lax.dot_general(
        left, right, (((1,), (1,)), ((), ())), preferred_element_type=jnp.float32
    )


def full_rows(values):
    return lax.all_gather(values, "col", axis=0, tiled=True)


def feature_sums(term):
    return lax.psum_scatter(
        term.astype(jnp.bfloat16), "col", scatter_dimension=0, tiled=True
    ).astype(jnp.float32)


def norm_forward(values, scale, shift):
    average = jnp.mean(values, axis=1, keepdims=True)
    meansq = jnp.mean(values * values, axis=1, keepdims=True)
    inverse = lax.rsqrt(meansq - average * average + epsilon)
    normed = (values - average) * inverse
    return (normed, inverse, (normed * scale + shift).astype(jnp.bfloat16))


def norm_backward(upper, normed, inverse, scale):
    scaled = upper * scale
    return inverse * (
        scaled
        - jnp.mean(scaled, axis=1, keepdims=True)
        - normed * jnp.mean(scaled * normed, axis=1, keepdims=True)
    )


def attend_forward(packed_img):
    images = packed_img.shape[0]
    head_dim = D // HEADS
    fields = packed_img.reshape(images, SEQ, 3, HEADS, head_dim)
    scores = jnp.einsum(
        "bqhd,bkhd->bhqk", fields[:, :, 0], fields[:, :, 1], preferred_element_type=jnp.float32
    ) * head_dim ** (-0.5)
    logsum = jnp.log(jnp.sum(jnp.exp(scores), axis=-1))
    prob_rows = jnp.exp(scores - logsum[..., None]).astype(jnp.bfloat16)
    mixed = jnp.einsum(
        "bhqk,bkhd->bqhd", prob_rows, fields[:, :, 2], preferred_element_type=jnp.float32
    )
    return (mixed.astype(jnp.bfloat16).reshape(images, SEQ, D), logsum)


def attend_backward(packed_img, logsum, grad_img):
    images = packed_img.shape[0]
    head_dim = D // HEADS
    factor = head_dim ** (-0.5)
    fields = packed_img.reshape(images, SEQ, 3, HEADS, head_dim)
    query_rows = fields[:, :, 0]
    key_rows = fields[:, :, 1]
    value_rows = fields[:, :, 2]
    grad_heads = grad_img.reshape(images, SEQ, HEADS, head_dim)
    scores = (
        jnp.einsum("bqhd,bkhd->bhqk", query_rows, key_rows, preferred_element_type=jnp.float32)
        * factor
    )
    probs_full = jnp.exp(scores - logsum[..., None])
    prob_rows = probs_full.astype(jnp.bfloat16)
    grad_probs = jnp.einsum(
        "bqhd,bkhd->bhqk", grad_heads, value_rows, preferred_element_type=jnp.float32
    )
    delta = jnp.sum(probs_full * grad_probs, axis=-1, keepdims=True)
    grad_scores = (probs_full * (grad_probs - delta) * factor).astype(jnp.bfloat16)
    grad_query = jnp.einsum(
        "bhqk,bkhd->bqhd", grad_scores, key_rows, preferred_element_type=jnp.float32
    )
    grad_key = jnp.einsum(
        "bhqk,bqhd->bkhd", grad_scores, query_rows, preferred_element_type=jnp.float32
    )
    grad_value = jnp.einsum(
        "bhqk,bqhd->bkhd", prob_rows, grad_heads, preferred_element_type=jnp.float32
    )
    stacked = jnp.stack([grad_query, grad_key, grad_value], axis=2)
    return stacked.reshape(images, SEQ, 3 * D).astype(jnp.bfloat16)


def body(
    tokens,
    packed,
    packed_bias,
    projection,
    projection_bias,
    expansion,
    expansion_bias,
    reduction,
    reduction_bias,
    first_scale,
    first_shift,
    second_scale,
    second_shift,
    upstream,
):
    groups = lax.axis_size("col")
    packed_full, projection_full, expansion_full, reduction_full = (
        lax.all_gather(packed, "dp", axis=0, tiled=True),
        lax.all_gather(projection, "dp", axis=1, tiled=True),
        lax.all_gather(expansion, "dp", axis=0, tiled=True),
        lax.all_gather(reduction, "dp", axis=1, tiled=True),
    )
    tokens_f = tokens.astype(jnp.float32)
    upstream_f = upstream.astype(jnp.float32)
    normed1, inverse1, rows1 = norm_forward(tokens_f, first_scale, first_shift)
    rows1_full = full_rows(rows1)
    count = rows1_full.shape[0]
    images = count // SEQ
    local = images // groups
    packed_rows = (
        jnp.dot(rows1_full, packed_full, preferred_element_type=jnp.float32) + packed_bias
    ).astype(jnp.bfloat16)
    received = lax.all_to_all(
        packed_rows.reshape(groups, local, SEQ, -1), "col", split_axis=0, concat_axis=3, tiled=True
    )
    mixed, logsum_img = attend_forward(received[0])
    scattered_img = lax.all_to_all(mixed[None], "col", split_axis=3, concat_axis=0, tiled=True)
    logsum = logsum_img[None]
    attn_rows = scattered_img.reshape(count, -1)
    resid = (
        tokens_f
        + feature_sums(jnp.dot(attn_rows, projection_full, preferred_element_type=jnp.float32))
        + projection_bias
    )
    normed2, inverse2, rows2 = norm_forward(resid, second_scale, second_shift)
    rows2_full = full_rows(rows2)
    hidden_pre = (
        jnp.dot(rows2_full, expansion_full, preferred_element_type=jnp.float32) + expansion_bias
    )
    hidden_act = jax.nn.gelu(hidden_pre, approximate=False).astype(jnp.bfloat16)
    layer_output = (
        resid
        + (
            feature_sums(jnp.dot(hidden_act, reduction_full, preferred_element_type=jnp.float32))
            + reduction_bias
        )
    ).astype(jnp.bfloat16)
    upstream_full = full_rows(upstream)
    reduction_bias_grad = jnp.sum(upstream_f, axis=0)
    reduction_grad = contract_rows(hidden_act, upstream_full)
    hidden_grad = contract_cols(upstream_full, reduction_full) * gelu_slope(hidden_pre)
    expansion_bias_grad = jnp.sum(hidden_grad, axis=0)
    hidden_grad_b = hidden_grad.astype(jnp.bfloat16)
    expansion_grad = contract_rows(rows2_full, hidden_grad_b)
    rows2_grad = feature_sums(contract_cols(hidden_grad_b, expansion_full))
    second_scale_grad = jnp.sum(rows2_grad * normed2, axis=0)
    second_shift_grad = jnp.sum(rows2_grad, axis=0)
    resid_grad = upstream_f + norm_backward(rows2_grad, normed2, inverse2, second_scale)
    projection_bias_grad = jnp.sum(resid_grad, axis=0)
    resid_grad_b = resid_grad.astype(jnp.bfloat16)
    resid_full = full_rows(resid_grad_b)
    projection_grad = contract_rows(attn_rows, resid_full)
    attn_grad = contract_cols(resid_full, projection_full).astype(jnp.bfloat16)
    grad_img = lax.all_to_all(
        attn_grad.reshape(groups, local, SEQ, -1), "col", split_axis=0, concat_axis=3, tiled=True
    )
    packed_grad_img = attend_backward(received[0], logsum[0], grad_img[0])
    packed_grad_rows = lax.all_to_all(
        packed_grad_img[None], "col", split_axis=3, concat_axis=0, tiled=True
    ).reshape(count, -1)
    packed_bias_grad = jnp.sum(packed_grad_rows.astype(jnp.float32), axis=0)
    packed_grad = contract_rows(rows1_full, packed_grad_rows)
    rows1_grad = feature_sums(contract_cols(packed_grad_rows, packed_full))
    first_scale_grad = jnp.sum(rows1_grad * normed1, axis=0)
    first_shift_grad = jnp.sum(rows1_grad, axis=0)
    input_grad = resid_grad + norm_backward(rows1_grad, normed1, inverse1, first_scale)
    feature_terms = jnp.stack(
        [
            projection_bias_grad,
            reduction_bias_grad,
            first_scale_grad,
            first_shift_grad,
            second_scale_grad,
            second_shift_grad,
        ],
        axis=0,
    )
    shares = lax.psum_scatter(feature_terms, "col", scatter_dimension=1, tiled=True)
    packed_grad, projection_grad, expansion_grad, reduction_grad = (
        lax.psum_scatter(
            packed_grad.astype(jnp.bfloat16), "dp", scatter_dimension=0, tiled=True
        ).astype(jnp.float32),
        lax.psum_scatter(
            projection_grad.astype(jnp.bfloat16), "dp", scatter_dimension=1, tiled=True
        ).astype(jnp.float32),
        lax.psum_scatter(
            expansion_grad.astype(jnp.bfloat16), "dp", scatter_dimension=0, tiled=True
        ).astype(jnp.float32),
        lax.psum_scatter(
            reduction_grad.astype(jnp.bfloat16), "dp", scatter_dimension=1, tiled=True
        ).astype(jnp.float32),
    )
    smalls = lax.psum(
        (
            packed_bias_grad,
            shares[0],
            expansion_bias_grad,
            shares[1],
            shares[2],
            shares[3],
            shares[4],
            shares[5],
        ),
        "dp",
    )
    return (
        layer_output,
        input_grad,
        packed_grad,
        projection_grad,
        expansion_grad,
        reduction_grad,
    ) + tuple(smalls)


def solution(mesh):
    placed = (
        P(("dp", "col"), None),
        P("dp", "col"),
        P("col"),
        P("col", "dp"),
        P(),
        P("dp", "col"),
        P("col"),
        P("col", "dp"),
        P(),
        P(),
        P(),
        P(),
        P(),
        P(("dp", "col"), None),
    )
    return jax.shard_map(
        body,
        mesh=mesh,
        in_specs=placed,
        out_specs=(
            P(("dp", "col"), None),
            P(("dp", "col"), None),
            P("dp", "col"),
            P("col", "dp"),
            P("dp", "col"),
            P("col", "dp"),
            P("col"),
            P("col"),
            P("col"),
            P("col"),
            P("col"),
            P("col"),
            P("col"),
            P("col"),
        ),
        check_vma=False,
    )
```

profile of v0, /device:TPU:0, one launch (start us, length us, event | category | flops | bytes accessed | tf_op | source)
XLA Modules:
  0.0 997.6 jit_solution(13019273879520020617)
XLA Ops:
  7.2 1.8 convert_reduce_fusion.1
  9.1 2.9 fusion.55
  12.0 32.6 %all_gather.25 = bf16[384,288]{1,0:T(8,128)(2,1)S(1)} all-gather(bf16[48,288]{1,0:T(8,128)(2,1)S(1)} %copy-done.16), channel_id=1, replica_groups=mesh['dp'=8,'col'=4] {'dp'}, dimensions={0}, use_global_device_ids=true | all-gather | bytes 248832 | tf_op jit(solution)/shard_map/all_gather | solution.py:126
  44.6 8.4 all-gather.5.cloned.1.call-done
  53.0 6.3 fusion.19
  59.3 15.9 %reshape.120 = bf16[4,8,197,288]{2,1,0,3:T(8,128)(2,1)} reshape(bf16[6304,288]{0,1:T(8,128)(2,1)} %fusion.19) | data formatting | bytes 7262208 | tf_op jit(solution)/shard_map/reshape | solution.py:142
  75.2 5.0 copy.77
  80.2 56.5 %all_to_all.60 = bf16[4,8,197,288]{2,3,1,0:T(8,128)(2,1)S(1)} all-to-all(bf16[4,8,197,288]{2,3,1,0:T(8,128)(2,1)S(1)} %copy.77), channel_id=1, replica_groups=mesh['dp'=8,'col'=4] {'col'}, dimensions={0} | all-to-all | bytes 7262208 | tf_op jit(solution)/shard_map/all_to_all | solution.py:141
  137.2 2.1 copy-done.4
  139.3 5.3 fusion.83
  144.5 10.6 %fusion.61 = bf16[8,6,64,197]{3,2,1,0:T(8,128)(2,1)S(1)} fusion(bf16[8,197,3,6,64]{1,4,3,2,0:T(8,128)(2,1)} %bitcast.97, f32[8,6,197,197]{2,3,1,0:T(8,128)} %fusion.83), kind=kOutput, calls=%fused_computation.93 | convolution fusion | flops 246508656 | bytes 22444032 | tf_op jit(solution)/shard_map/bhqk,bkhd->bqhd/dot_general | solution.py:69
  155.1 2.0 copy.83
  157.1 3.6 all-to-all-start.1
  160.8 30.9 %all_gather.26 = bf16[96,384]{0,1:T(8,128)(2,1)S(1)} all-gather(bf16[96,48]{0,1:T(8,128)(2,1)S(1)} %copy-done.22), channel_id=1, replica_groups=mesh['dp'=8,'col'=4] {'dp'}, dimensions={1}, use_global_device_ids=true | all-gather | bytes 82944 | tf_op jit(solution)/shard_map/all_gather | solution.py:127
  192.8 5.4 copy.99
  198.3 5.1 copy.85
  203.4 3.3 reshape.121
  206.7 3.8 convolution_convert_fusion.3
  210.6 50.5 %reduce-scatter.30.cloned.1.call-done = bf16[1576,384]{1,0:T(8,128)(2,1)} async-done(((bf16[6304,384]{1,0:T(8,128)(2,1)}), bf16[1576,384]{1,0:T(8,128)(2,1)}) %reduce-scatter.30.cloned.1.call-update) | async-done | bytes 1210384
  261.1 2.0 fusion.87
  263.1 3.0 add_convert_fusion.1
  266.8 31.0 %all_gather.28 = bf16[384,384]{1,0:T(8,128)(2,1)S(1)} all-gather(bf16[48,384]{1,0:T(8,128)(2,1)S(1)} %copy-done.17), channel_id=1, replica_groups=mesh['dp'=8,'col'=4] {'dp'}, dimensions={0}, use_global_device_ids=true | all-gather | bytes 331776 | tf_op jit(solution)/shard_map/all_gather | solution.py:128
  297.8 41.8 %all_gather.29 = bf16[384,384]{0,1:T(8,128)(2,1)S(1)} all-gather(bf16[384,48]{0,1:T(8,128)(2,1)S(1)} %copy-done.18), channel_id=1, replica_groups=mesh['dp'=8,'col'=4] {'dp'}, dimensions={1}, use_global_device_ids=true | all-gather | bytes 331776 | tf_op jit(solution)/shard_map/all_gather | solution.py:129
  339.6 26.5 %fusion.7 = (bf16[6304,384]{1,0:T(8,128)(2,1)}, f32[6304,384]{1,0:T(8,128)}) fusion(f32[384]{0:T(512)S(1)} %copy-done.26, bf16[6304,384]{1,0:T(8,128)(2,1)} %all-gather.7.cloned.1.call-done, bf16[384,384]{1,0:T(8,128)(2,1)S(1)} %all_gather.28), kind=kOutput, calls=%fused_computation.20 | convolution fusion | flops 2018893824 | bytes 19662336 | tf_op jit(solution)/shard_map/dot_general | solution.py:156
  366.1 9.1 fusion.109
  375.2 2.1 copy-done.1
  377.3 5.2 convolution_convert_fusion.1
  382.6 7.7 convolution_convert_fusion.2
  390.4 41.5 %reduce-scatter.34.cloned.1.call-done = bf16[1576,384]{1,0:T(8,128)(2,1)} async-done(((bf16[6304,384]{1,0:T(8,128)(2,1)}), bf16[1576,384]{1,0:T(8,128)(2,1)}) %reduce-scatter.34.cloned.1.call-update) | async-done | bytes 1210384
  431.9 2.8 fusion.49
  434.7 48.7 %reduce-scatter.32.cloned.1.call-done = bf16[1576,384]{1,0:T(8,128)(2,1)} async-done(((bf16[6304,384]{1,0:T(8,128)(2,1)}), bf16[1576,384]{1,0:T(8,128)(2,1)}) %reduce-scatter.32.cloned.1.call-update) | async-done | bytes 1210384
  483.5 4.7 fusion.107
  490.8 38.3 %all-gather.11.cloned.1.call-done = bf16[6304,384]{1,0:T(8,128)(2,1)} async-done(((bf16[1576,384]{1,0:T(8,128)(2,1)}), bf16[6304,384]{1,0:T(8,128)(2,1)}) %all-gather.11.cloned.1.call-update) | async-done | bytes 4841488 | tf_op jit(solution)/shard_map/all_gather | solution.py:34
  529.1 4.0 convolution_convert_fusion.4
  533.1 5.6 reshape.122
  538.7 2.7 copy.86
  541.4 4.0 all-to-all-start.2
  545.4 13.2 %fusion.2 = f32[8,6,197,197]{2,3,1,0:T(8,128)} fusion(f32[8,6,197,197]{2,3,1,0:T(8,128)} %fusion.83), kind=kOutput, calls=%fused_computation.8 | output fusion | flops 5598148 | bytes 14902656 | tf_op jit(solution)/shard_map/reduce_sum | solution.py:67
  558.6 6.4 all-to-all-done.2
  566.5 11.7 %fusion.79 = bf16[8,197,1,6,64]{1,4,3,0,2:T(8,128)(2,1)} fusion(bf16[8,197,6,64]{1,3,2,0:T(8,128)(2,1)} %bitcast.105, f32[8,6,197,197]{2,3,1,0:T(8,128)} %fusion.83), kind=kOutput, calls=%fused_computation.102 | convolution fusion | flops 246508656 | bytes 9872064 | tf_op jit(solution)/shard_map/bhqk,bqhd->bkhd/dot_general | solution.py:101
  578.2 6.7 fusion.82
  584.9 16.6 %fusion.76 = bf16[8,197,1,6,64]{1,4,3,0,2:T(8,128)(2,1)} fusion(f32[8,6,197,197]{2,3,1,0:T(8,128)} %fusion.2, f32[8,6,197,197]{2,3,1,0:T(8,128)} %fusion.82, bf16[8,197,3,6,64]{1,4,3,2,0:T(8,128)(2,1)} %bitcast.99), kind=kOutput, calls=%fused_computation.101 | convolution fusion | flops 248371488 | bytes 42104832 | tf_op jit(solution)/shard_map/bhqk,bkhd->bqhd/dot_general | solution.py:95
  601.4 16.9 %fusion.73 = bf16[8,197,1,6,64]{1,4,3,0,2:T(8,128)(2,1)} fusion(f32[8,6,197,197]{2,3,1,0:T(8,128)} %fusion.2, f32[8,6,197,197]{2,3,1,0:T(8,128)} %fusion.82, bf16[8,197,3,6,64]{1,4,3,2,0:T(8,128)(2,1)} %bitcast.100), kind=kOutput, calls=%fused_computation.100 | convolution fusion | flops 248371488 | bytes 42104832 | tf_op jit(solution)/shard_map/bhqk,bqhd->bkhd/dot_general | solution.py:98
  618.3 2.5 pad_maximum_fusion
  621.5 12.9 %copy.92 = bf16[1,8,197,1152]{2,1,0,3:T(8,128)(2,1)} copy(bf16[1,8,197,1152]{2,3,1,0:T(8,128)(2,1)S(1)} %bitcast.101) | data formatting | bytes 7262208 | tf_op jit(solution)/shard_map/convert_element_type | solution.py:105
  634.4 5.0 all-to-all-start.3
  639.4 7.3 convolution_convert_fusion.5
  647.0 7.3 fusion.84
  654.5 5.1 convolution_convert_fusion.7
  659.6 33.6 %all-to-all-done.3 = bf16[1,8,197,1152]{2,1,0,3:T(8,128)(2,1)} async-done(((bf16[1,8,197,1152]{2,1,0,3:T(8,128)(2,1)}), bf16[1,8,197,1152]{2,1,0,3:T(8,128)(2,1)}, u32[]{:S(2)}, u32[]{:S(2)}) %all-to-all-start.3) | async-done | bytes 3631136 | tf_op jit(solution)/shard_map/all_to_all | solution.py:186
  693.2 12.9 %copy.100 = bf16[1,8,197,4,288]{4,3,1,2,0:T(4,128)(2,1)} copy(bf16[1,8,197,4,288]{2,1,4,3,0:T(8,128)(2,1)} %bitcast.22) | data formatting | bytes 7262208 | tf_op jit(solution)/shard_map/all_to_all | solution.py:186
  706.1 14.4 %copy.94 = bf16[4,1,8,197,288]{3,2,0,4,1:T(8,128)(2,1)} copy(bf16[4,1,8,197,288]{4,0,2,3,1:T(4,128)(2,1)} %bitcast.95) | data formatting | bytes 7262208 | tf_op jit(solution)/shard_map/all_to_all | solution.py:186
  720.5 9.2 reshape.123
  729.7 7.0 convolution_convert_fusion.6
  737.0 7.5 convolution_convert_fusion
  746.0 23.8 %reduce-scatter.24.cloned.1.call-done = bf16[48,384]{1,0:T(8,128)(2,1)} async-done(((bf16[384,384]{1,0:T(8,128)(2,1)}), bf16[48,384]{1,0:T(8,128)(2,1)}) %reduce-scatter.24.cloned.1.call-update) | async-done | bytes 36880 | tf_op jit(solution)/shard_map/reduce_scatter | solution.py:214
  771.2 59.5 %reduce-scatter.22.cloned.1.call-done = bf16[96,48]{0,1:T(8,128)(2,1)} async-done(((bf16[96,384]{0,1:T(8,128)(2,1)}), bf16[96,48]{0,1:T(8,128)(2,1)}) %reduce-scatter.22.cloned.1.call-update) | async-done | bytes 9232 | tf_op jit(solution)/shard_map/reduce_scatter | solution.py:211
  832.0 4.6 convert_reduce_fusion
  836.7 56.0 %reduce-scatter.20.cloned.1.call-done = bf16[48,288]{1,0:T(8,128)(2,1)} async-done(((bf16[384,288]{1,0:T(8,128)(2,1)}), bf16[48,288]{1,0:T(8,128)(2,1)}) %reduce-scatter.20.cloned.1.call-update) | async-done | bytes 27664 | tf_op jit(solution)/shard_map/reduce_scatter | solution.py:208
  894.0 49.1 %reduce-scatter.36.cloned.1.call-done = bf16[1576,384]{1,0:T(8,128)(2,1)} async-done(((bf16[6304,384]{1,0:T(8,128)(2,1)}), bf16[1576,384]{1,0:T(8,128)(2,1)}) %reduce-scatter.36.cloned.1.call-update) | async-done | bytes 1210384
  943.2 2.7 fusion.50
  946.8 3.7 fusion.44
  950.5 16.3 %reduce-scatter.28.cloned.1.call-done = f32[96,6]{1,0:T(8,128)} async-done(((f32[384,6]{1,0:T(8,128)}), f32[96,6]{1,0:T(8,128)}) %reduce-scatter.28.cloned.1.call-update) | async-done | bytes 2320
  968.4 22.2 %all-reduce.4 = (f32[288]{0:T(512)}, f32[96]{0:T(128)}, f32[384]{0:T(512)}, f32[96]{0:T(128)}, f32[96]{0:T(128)}, /*index=5*/f32[96]{0:T(128)}, f32[96]{0:T(128)}, f32[96]{0:T(128)}) all-reduce(f32[288]{0:T(512)S(1)} %convert_reduce_fusion, f32[96]{0:T(128)S(1)} %bitcast.115, ...), channel_id=1, replica_groups=mesh['dp'=8,'col'=4] {'dp'}, use_global_device_ids=true, to_apply=%region_19.0 | all-reduce | flops 1248 | bytes 9984 | tf_op jit(solution)/shard_map/psum | solution.py:221
  (110 shorter events, 16.3 us)
Async XLA Ops:
  7.2 4.8 copy-start.16
  7.2 45.8 %copy-start.25 = (f32[288]{0:T(512)S(1)}, f32[288]{0:T(512)}, u32[]{:S(2)}) copy-start(f32[288]{0:T(512)} %param.16) | copy-start | bytes 3460
  7.2 45.8 %all-gather.5.cloned.1.call-start = ((), (), s32[]{:S(2)}) async-start(), calls=%async_computation.13 | async-start | bytes 6051840 | tf_op jit(solution)/shard_map/all_gather | solution.py:34
  9.1 2.9 copy-start.12
  9.1 2.9 copy-start.14
  44.6 14.7 %copy-start.10 = (bf16[384,288]{1,0:T(8,128)(2,1)}, bf16[384,288]{1,0:T(8,128)(2,1)S(1)}, u32[]{:S(2)}) copy-start(bf16[384,288]{1,0:T(8,128)(2,1)S(1)} %all_gather.25) | copy-start | bytes 663556
  137.2 2.1 copy-start.4
  155.1 5.7 copy-start.22
  157.1 34.6 %all-to-all-start.1 = ((bf16[1,8,197,384]{2,1,0,3:T(8,128)(2,1)}), bf16[1,8,197,384]{2,1,0,3:T(8,128)(2,1)S(1)}, u32[]{:S(2)}, u32[]{:S(2)}) async-start(bf16[1,8,197,384]{2,1,0,3:T(8,128)(2,1)} %copy.83), calls=%async_computation.1 | async-start | bytes 3145728 | tf_op jit(solution)/shard_map/all_to_all | solution.py:145
  160.7 100.4 %reduce-scatter.30.cloned.1.call-start = ((), (), s32[]{:S(2)}) async-start(), calls=%async_computation.22 | async-start | bytes 6051840
  191.7 1.1 copy-start.7
  206.7 3.8 copy-start.5
  210.5 50.6 %copy-start = (bf16[1576,384]{1,0:T(8,128)(2,1)S(1)}, bf16[1576,384]{1,0:T(8,128)(2,1)}, u32[]{:S(2)}) copy-start(bf16[1576,384]{1,0:T(8,128)(2,1)} %param.14) | copy-start | bytes 3631108
  210.5 50.6 %copy-start.19 = (f32[384]{0:T(512)S(1)}, f32[384]{0:T(512)}, u32[]{:S(2)}) copy-start(f32[384]{0:T(512)} %param.18) | copy-start | bytes 4612
  210.5 52.6 %copy-start.20 = (f32[384]{0:T(512)S(1)}, f32[384]{0:T(512)}, u32[]{:S(2)}) copy-start(f32[384]{0:T(512)} %param.25) | copy-start | bytes 4612
  210.5 52.6 %copy-start.23 = (f32[384]{0:T(512)S(1)}, f32[384]{0:T(512)}, u32[]{:S(2)}) copy-start(f32[384]{0:T(512)} %param.26) | copy-start | bytes 4612
  210.6 56.2 %copy-start.17 = (bf16[48,384]{1,0:T(8,128)(2,1)S(1)}, bf16[48,384]{1,0:T(8,128)(2,1)}, u32[]{:S(2)}) copy-start(bf16[48,384]{1,0:T(8,128)(2,1)} %param.19) | copy-start | bytes 110596
  210.6 87.2 %copy-start.18 = (bf16[384,48]{0,1:T(8,128)(2,1)S(1)}, bf16[384,48]{0,1:T(8,128)(2,1)}, u32[]{:S(2)}) copy-start(bf16[384,48]{0,1:T(8,128)(2,1)} %param.21) | copy-start | bytes 110596
  210.6 129.0 %copy-start.26 = (f32[384]{0:T(512)S(1)}, f32[384]{0:T(512)}, u32[]{:S(2)}) copy-start(f32[384]{0:T(512)} %param.20) | copy-start | bytes 4612
  210.6 129.0 %all-gather.7.cloned.1.call-start = ((), (), s32[]{:S(2)}) async-start(), calls=%async_computation.14 | async-start | bytes 6051840 | tf_op jit(solution)/shard_map/all_gather | solution.py:34
  266.2 99.9 %all-gather.9.cloned.1.call-start = ((), (), s32[]{:S(2)}) async-start(), calls=%async_computation.15 | async-start | bytes 6051840 | tf_op jit(solution)/shard_map/all_gather | solution.py:34
  266.7 165.2 %reduce-scatter.34.cloned.1.call-start = ((), (), s32[]{:S(2)}) async-start(), calls=%async_computation.24 | async-start | bytes 6051840
  375.2 2.2 copy-start.1
  382.6 100.9 %reduce-scatter.32.cloned.1.call-start = ((), (), s32[]{:S(2)}) async-start(), calls=%async_computation.23 | async-start | bytes 6051840
  390.3 41.6 %copy-start.3 = (bf16[1576,384]{1,0:T(8,128)(2,1)S(1)}, bf16[1576,384]{1,0:T(8,128)(2,1)}, u32[]{:S(2)}) copy-start(bf16[1576,384]{1,0:T(8,128)(2,1)} %reduce-scatter.30.cloned.1.call-done) | copy-start | bytes 3631108
  390.3 93.2 %copy-start.24 = (f32[384]{0:T(512)S(1)}, f32[384]{0:T(512)}, u32[]{:S(2)}) copy-start(f32[384]{0:T(512)} %param.22) | copy-start | bytes 4612
  390.3 138.8 %all-gather.11.cloned.1.call-start = ((), (), s32[]{:S(2)}) async-start(), calls=%async_computation.16 | async-start | bytes 6051840 | tf_op jit(solution)/shard_map/all_gather | solution.py:34
  488.1 1.4 copy-start.2
  541.4 23.6 %all-to-all-start.2 = ((bf16[4,8,197,96]{2,1,3,0:T(8,128)(2,1)}), bf16[4,8,197,96]{2,1,3,0:T(8,128)(2,1)S(1)}, u32[]{:S(2)}, u32[]{:S(2)}) async-start(bf16[4,8,197,96]{2,1,3,0:T(8,128)(2,1)} %copy.86), calls=%async_computation.2 | async-start | bytes 3145728 | tf_op jit(solution)/shard_map/all_to_all | solution.py:182
  566.5 11.7 %copy-start.8 = (bf16[1,8,197,4,96]{2,4,3,1,0:T(8,128)(2,1)S(1)}, bf16[1,8,197,4,96]{2,4,3,1,0:T(8,128)(2,1)}, u32[]{:S(2)}) copy-start(bf16[1,8,197,4,96]{2,4,3,1,0:T(8,128)(2,1)} %copy.87) | copy-start | bytes 3631108
  601.4 16.9 %copy-start.9 = (bf16[8,197,1,6,64]{1,4,3,0,2:T(8,128)(2,1)S(1)}, bf16[8,197,1,6,64]{1,4,3,0,2:T(8,128)(2,1)}, u32[]{:S(2)}) copy-start(bf16[8,197,1,6,64]{1,4,3,0,2:T(8,128)(2,1)} %fusion.79) | copy-start | bytes 3631108
  634.4 58.8 %all-to-all-start.3 = ((bf16[1,8,197,1152]{2,1,0,3:T(8,128)(2,1)}), bf16[1,8,197,1152]{2,1,0,3:T(8,128)(2,1)}, u32[]{:S(2)}, u32[]{:S(2)}) async-start(bf16[1,8,197,1152]{2,1,0,3:T(8,128)(2,1)} %copy.92), calls=%async_computation.3 | async-start | bytes 9437184 | tf_op jit(solution)/shard_map/all_to_all | solution.py:186
  639.4 105.2 %reduce-scatter.26.cloned.1.call-start = ((), (), s32[]{:S(2)}) async-start(), calls=%async_computation.20 | async-start | bytes 331776 | tf_op jit(solution)/shard_map/reduce_scatter | solution.py:217
  646.8 7.7 copy-start.6
  646.8 123.0 %reduce-scatter.24.cloned.1.call-start = ((), (), s32[]{:S(2)}) async-start(), calls=%async_computation.19 | async-start | bytes 331776 | tf_op jit(solution)/shard_map/reduce_scatter | solution.py:214
  654.4 176.3 %reduce-scatter.22.cloned.1.call-start = ((), (), s32[]{:S(2)}) async-start(), calls=%async_computation.18 | async-start | bytes 110592 | tf_op jit(solution)/shard_map/reduce_scatter | solution.py:211
  659.6 233.1 %reduce-scatter.20.cloned.1.call-start = ((), (), s32[]{:S(2)}) async-start(), calls=%async_computation.17 | async-start | bytes 331776 | tf_op jit(solution)/shard_map/reduce_scatter | solution.py:208
  729.7 7.4 copy-start.11
  736.7 206.5 %reduce-scatter.36.cloned.1.call-start = ((), (), s32[]{:S(2)}) async-start(), calls=%async_computation.25 | async-start | bytes 6051840
  744.5 198.7 %copy-start.13 = (f32[1576]{0:T(1024)S(1)}, f32[1576]{0:T(1024)}, u32[]{:S(2)}) copy-start(f32[1576]{0:T(1024)} %copy-done.12) | copy-start | bytes 18916
  744.5 198.7 %copy-start.15 = (f32[1576]{0:T(1024)S(1)}, f32[1576]{0:T(1024)}, u32[]{:S(2)}) copy-start(f32[1576]{0:T(1024)} %copy-done.14) | copy-start | bytes 18916
  744.5 198.7 %copy-start.21 = (f32[384]{0:T(512)S(1)}, f32[384]{0:T(512)}, u32[]{:S(2)}) copy-start(f32[384]{0:T(512)} %param.23) | copy-start | bytes 4612
  744.5 222.2 %reduce-scatter.28.cloned.1.call-start = ((), (), s32[]{:S(2)}) async-start(), calls=%async_computation.21 | async-start | bytes 245760
Sparse Core Ops, SparseCore 0:
  12.1 40.8 all-gather.4
  210.7 50.3 reduce-scatter.29
  266.3 38.1 all-gather.6
  305.8 38.1 all-gather.8
  382.7 49.1 reduce-scatter.33
  434.4 49.0 reduce-scatter.31
  490.9 38.1 all-gather.10
  646.9 60.9 reduce-scatter.25
  711.2 58.5 reduce-scatter.23
  772.9 57.7 reduce-scatter.21
  834.0 58.5 reduce-scatter.19
  895.1 48.0 reduce-scatter.35
  946.9 19.7 reduce-scatter.27
where the time goes:
time: 1010 us; the launch traced here: 998 us
  waiting for transfers between devices  433 us (43%)
  blocking collectives  215 us (21%)
  matrix products  164 us (16%)
  local copies, waits for them, and re-layouts  106 us (10%)
  other arithmetic  50.6 us (5%)
  between operations  14.7 us (1%)
  starting transfers between devices  13.5 us (1%)
    unnamed x18, waiting for transfers between devices  207 us
    reduce_scatter x1, waiting for transfers between devices, body(): lax.psum_scatter(projection_grad.astype(jnp.bfloat16), 'dp', scatter_dime...  59.5 us
    all_to_all x1, blocking collectives, body(): lax.all_to_all(packed_rows.reshape(groups, local, SEQ, -1), 'col', split_...  56.5 us
    reduce_scatter x1, waiting for transfers between devices, body(): lax.psum_scatter(packed_grad.astype(jnp.bfloat16), 'dp', scatter_dimensio...  56 us
    all_gather x4, waiting for transfers between devices, full_rows(): return lax.all_gather(values, 'col', axis=0, tiled=True)  46.7 us
    all_gather x1, blocking collectives, body(): lax.all_gather(reduction, 'dp', axis=1, tiled=True)  41.8 us
    all_to_all x1, waiting for transfers between devices, body(): lax.all_to_all(packed_grad_img[None], 'col', split_axis=3, concat_axis=0,...  33.6 us
    all_gather x1, blocking collectives, body(): lax.all_gather(packed, 'dp', axis=0, tiled=True)  32.6 us
  transfers between devices with their start and end apart: 16, of which 12 were waited for; matrix products, arithmetic and copies ran while one was open for 14% of the time, Pallas kernels for 0%

commit v1 on v0

--- a/solution.py
+++ b/solution.py
@@ -9,6 +9,36 @@
 epsilon = 1e-06
 root_half = 0.7071067811865476
 inv_root_tau = 0.3989422804014327
+
+
+def watch_the_series_all(work_x, along_dim, patch):
+    carry, carry_in = (work_x.shape[:along_dim], work_x.shape[along_dim + 1 :])
+    even = work_x.reshape(*carry, patch, -1, *carry_in)
+    return jnp.moveaxis(even, along_dim, 0)
+
+
+def _draw_circles(vec, d_out):
+    vec = jnp.moveaxis(vec, 0, d_out)
+    view_out = vec.shape
+    return vec.reshape(
+        *view_out[:d_out], view_out[d_out] * view_out[d_out + 1], *view_out[d_out + 2 :]
+    )
+
+
+def touch_boxes(arr_in, ax_name, u_in, payload):
+    w_next = lax.axis_size(ax_name)
+    built = lax.axis_index(ax_name)
+    heard, fresh = (w_next, built)
+    mixed_arr = watch_the_series_all(arr_in, u_in, heard)
+    w1 = mixed_arr
+    for ii in range(1, heard):
+        z, e_now = ((fresh + ii) % heard, (fresh - ii) % heard)
+        mat_out = lax.dynamic_index_in_dim(mixed_arr, z, 0)
+        u_next = lax.ppermute(
+            mat_out, axis_name=ax_name, perm=[(w, (w + ii) % heard) for w in range(heard)]
+        )
+        w1 = lax.dynamic_update_slice_in_dim(w1, u_next, e_now, axis=0)
+    return _draw_circles(w1, payload)
 
 
 def gelu_slope(values):
@@ -138,9 +168,7 @@
     packed_rows = (
         jnp.dot(rows1_full, packed_full, preferred_element_type=jnp.float32) + packed_bias
     ).astype(jnp.bfloat16)
-    received = lax.all_to_all(
-        packed_rows.reshape(groups, local, SEQ, -1), "col", split_axis=0, concat_axis=3, tiled=True
-    )
+    received = touch_boxes(packed_rows.reshape(groups, local, SEQ, -1), "col", 0, 3)
     mixed, logsum_img = attend_forward(received[0])
     scattered_img = lax.all_to_all(mixed[None], "col", split_axis=3, concat_axis=0, tiled=True)
     logsum = logsum_img[None]

time: 1010 us -> 1010 us (level)
  blocking collectives: 215 us -> 159 us
  waiting for transfers between devices: 433 us -> 479 us
    all_to_all x1 -> x0, blocking collectives: 56.5 us -> none  [body(): lax.all_to_all(packed_rows.reshape(groups, local, SEQ, -1), 'col', split_...]
    ppermute x0 -> x3, waiting for transfers between devices: none -> 46.2 us  [touch_boxes(): lax.ppermute(mat_out, axis_name=ax_name, perm=[(w, (w + ii) % heard) for...]
    another operation x0 -> x2, local copies, waits for them, and re-layouts: none -> 20.9 us  [watch_the_series_all(): even = work_x.reshape(*carry, patch, -1, *carry_in)]
    reshape x2 -> x0, local copies, waits for them, and re-layouts: 20.9 us -> none  [body(): packed_rows.reshape(groups, local, SEQ, -1)]
  transfers between devices with their start and end apart: 16 -> 19, of which waited for: 12 -> 14; matrix products, arithmetic and copies ran while one was open for 14% -> 14% of each run, Pallas kernels for 0% -> 0%
where the time goes in v1:
time: 1010 us; the launch traced here: 997 us
  waiting for transfers between devices  479 us (47%)
  matrix products  166 us (16%)
  blocking collectives  159 us (16%)
  local copies, waits for them, and re-layouts  113 us (11%)
  other arithmetic  50.6 us (5%)
  starting transfers between devices  15.5 us (2%)
  between operations  14.8 us (1%)
    unnamed x18, waiting for transfers between devices  207 us
    reduce_scatter x1, waiting for transfers between devices, body(): lax.psum_scatter(projection_grad.astype(jnp.bfloat16), 'dp', scatter_dime...  59.5 us
    reduce_scatter x1, waiting for transfers between devices, body(): lax.psum_scatter(packed_grad.astype(jnp.bfloat16), 'dp', scatter_dimensio...  55.9 us
    all_gather x4, waiting for transfers between devices, full_rows(): return lax.all_gather(values, 'col', axis=0, tiled=True)  46.6 us
    ppermute x3, waiting for transfers between devices, touch_boxes(): lax.ppermute(mat_out, axis_name=ax_name, perm=[(w, (w + ii) % heard) for...  46.2 us
    all_gather x1, blocking collectives, body(): lax.all_gather(reduction, 'dp', axis=1, tiled=True)  41.8 us
    all_to_all x1, waiting for transfers between devices, body(): lax.all_to_all(packed_grad_img[None], 'col', split_axis=3, concat_axis=0,...  33.6 us
    all_gather x1, blocking collectives, body(): lax.all_gather(packed, 'dp', axis=0, tiled=True)  32.6 us
  transfers between devices with their start and end apart: 19, of which 14 were waited for; matrix products, arithmetic and copies ran while one was open for 14% of the time, Pallas kernels for 0%

profile of v1, /device:TPU:0, one launch (start us, length us, event | category | flops | bytes accessed | tf_op | source)
XLA Modules:
  0.0 997.3 jit_solution(9960602967597587970)
XLA Ops:
  9.1 2.9 fusion.55
  12.1 32.6 %all_gather.25 = bf16[384,288]{1,0:T(8,128)(2,1)S(1)} all-gather(bf16[48,288]{1,0:T(8,128)(2,1)S(1)} %copy-done.16), channel_id=1, replica_groups=mesh['dp'=8,'col'=4] {'dp'}, dimensions={0}, use_global_device_ids=true | all-gather | bytes 248832 | tf_op jit(solution)/shard_map/all_gather | solution.py:156
  44.7 8.3 all-gather.5.cloned.1.call-done
  53.0 6.3 fusion.19
  59.3 15.9 %reshape_reshape.3 = bf16[4,1,8,197,288]{3,2,0,4,1:T(8,128)(2,1)} reshape(bf16[6304,288]{0,1:T(8,128)(2,1)} %fusion.19) | data formatting | bytes 7262208 | tf_op jit(solution)/shard_map/reshape;reshape | solution.py:16
  75.2 5.0 copy.86
  80.3 2.1 copy-done.2
  86.3 25.8 %collective-permute-done = bf16[1,1,8,197,288]{3,4,0,2,1:T(8,128)(2,1)} collective-permute-done((bf16[1,1,8,197,288]{3,4,0,2,1:T(8,128)(2,1)}, bf16[1,1,8,197,288]{3,4,0,2,1:T(8,128)(2,1)}, u32[]{:S(2)}, u32[]{:S(2)}) %collective-permute-start) | collective-permute-done | bytes 907808 | tf_op jit(solution)/shard_map/ppermute | solution.py:37
  112.0 2.4 constant_dynamic-update-slice_fusion.2
  115.6 20.4 %collective-permute-done.2 = bf16[1,1,8,197,288]{3,4,0,2,1:T(8,128)(2,1)S(1)} collective-permute-done((bf16[1,1,8,197,288]{3,4,0,2,1:T(8,128)(2,1)}, bf16[1,1,8,197,288]{3,4,0,2,1:T(8,128)(2,1)S(1)}, u32[]{:S(2)}, u32[]{:S(2)}) %collective-permute-start.2) | collective-permute-done | bytes 907808 | tf_op jit(solution)/shard_map/ppermute | solution.py:37
  137.1 7.2 fusion.83
  144.3 10.6 %fusion.61 = bf16[8,6,64,197]{3,2,1,0:T(8,128)(2,1)S(1)} fusion(bf16[8,197,3,6,64]{1,4,3,2,0:T(8,128)(2,1)} %bitcast.95, f32[8,6,197,197]{2,3,1,0:T(8,128)} %fusion.83), kind=kOutput, calls=%fused_computation.93 | convolution fusion | flops 246508656 | bytes 22444032 | tf_op jit(solution)/shard_map/bhqk,bkhd->bqhd/dot_general | solution.py:99
  154.8 2.0 copy.93
  156.9 3.6 all-to-all-start
  160.5 31.1 %all_gather.26 = bf16[96,384]{0,1:T(8,128)(2,1)S(1)} all-gather(bf16[96,48]{0,1:T(8,128)(2,1)S(1)} %copy-done.22), channel_id=1, replica_groups=mesh['dp'=8,'col'=4] {'dp'}, dimensions={1}, use_global_device_ids=true | all-gather | bytes 82944 | tf_op jit(solution)/shard_map/all_gather | solution.py:157
  192.8 5.4 copy.109
  198.2 5.1 copy.95
  203.4 3.3 reshape.116
  206.7 3.8 convolution_convert_fusion.3
  210.6 50.4 %reduce-scatter.30.cloned.1.call-done = bf16[1576,384]{1,0:T(8,128)(2,1)} async-done(((bf16[6304,384]{1,0:T(8,128)(2,1)}), bf16[1576,384]{1,0:T(8,128)(2,1)}) %reduce-scatter.30.cloned.1.call-update) | async-done | bytes 1210384
  263.1 3.0 add_convert_fusion.1
  266.7 31.0 %all_gather.28 = bf16[384,384]{1,0:T(8,128)(2,1)S(1)} all-gather(bf16[48,384]{1,0:T(8,128)(2,1)S(1)} %copy-done.17), channel_id=1, replica_groups=mesh['dp'=8,'col'=4] {'dp'}, dimensions={0}, use_global_device_ids=true | all-gather | bytes 331776 | tf_op jit(solution)/shard_map/all_gather | solution.py:158
  297.7 41.8 %all_gather.29 = bf16[384,384]{0,1:T(8,128)(2,1)S(1)} all-gather(bf16[384,48]{0,1:T(8,128)(2,1)S(1)} %copy-done.18), channel_id=1, replica_groups=mesh['dp'=8,'col'=4] {'dp'}, dimensions={1}, use_global_device_ids=true | all-gather | bytes 331776 | tf_op jit(solution)/shard_map/all_gather | solution.py:159
  339.5 26.5 %fusion.7 = (bf16[6304,384]{1,0:T(8,128)(2,1)}, f32[6304,384]{1,0:T(8,128)}) fusion(f32[384]{0:T(512)S(1)} %copy-done.26, bf16[6304,384]{1,0:T(8,128)(2,1)} %all-gather.7.cloned.1.call-done, bf16[384,384]{1,0:T(8,128)(2,1)S(1)} %all_gather.28), kind=kOutput, calls=%fused_computation.20 | convolution fusion | flops 2018893824 | bytes 19662336 | tf_op jit(solution)/shard_map/dot_general | solution.py:184
  366.0 9.1 fusion.109
  375.2 2.1 copy-done.1
  377.3 5.2 convolution_convert_fusion.1
  382.6 7.7 convolution_convert_fusion.2
  390.4 41.5 %reduce-scatter.34.cloned.1.call-done = bf16[1576,384]{1,0:T(8,128)(2,1)} async-done(((bf16[6304,384]{1,0:T(8,128)(2,1)}), bf16[1576,384]{1,0:T(8,128)(2,1)}) %reduce-scatter.34.cloned.1.call-update) | async-done | bytes 1210384
  431.9 2.8 fusion.49
  434.7 48.7 %reduce-scatter.32.cloned.1.call-done = bf16[1576,384]{1,0:T(8,128)(2,1)} async-done(((bf16[6304,384]{1,0:T(8,128)(2,1)}), bf16[1576,384]{1,0:T(8,128)(2,1)}) %reduce-scatter.32.cloned.1.call-update) | async-done | bytes 1210384
  483.4 4.7 fusion.107
  490.7 38.3 %all-gather.11.cloned.1.call-done = bf16[6304,384]{1,0:T(8,128)(2,1)} async-done(((bf16[1576,384]{1,0:T(8,128)(2,1)}), bf16[6304,384]{1,0:T(8,128)(2,1)}) %all-gather.11.cloned.1.call-update) | async-done | bytes 4841488 | tf_op jit(solution)/shard_map/all_gather | solution.py:64
  529.0 4.0 convolution_convert_fusion.4
  533.0 5.6 reshape.117
  538.6 2.7 copy.96
  541.3 4.0 all-to-all-start.1
  545.3 13.2 %fusion.2 = f32[8,6,197,197]{2,3,1,0:T(8,128)} fusion(f32[8,6,197,197]{2,3,1,0:T(8,128)} %fusion.83), kind=kOutput, calls=%fused_computation.8 | output fusion | flops 5598148 | bytes 14902656 | tf_op jit(solution)/shard_map/reduce_sum | solution.py:97
  558.5 6.4 all-to-all-done.1
  566.4 11.7 %fusion.79 = bf16[8,197,1,6,64]{1,4,3,0,2:T(8,128)(2,1)} fusion(bf16[8,197,6,64]{1,3,2,0:T(8,128)(2,1)} %bitcast.103, f32[8,6,197,197]{2,3,1,0:T(8,128)} %fusion.83), kind=kOutput, calls=%fused_computation.102 | convolution fusion | flops 246508656 | bytes 9872064 | tf_op jit(solution)/shard_map/bhqk,bqhd->bkhd/dot_general | solution.py:131
  578.1 6.7 fusion.82
  584.8 16.6 %fusion.76 = bf16[8,197,1,6,64]{1,4,3,0,2:T(8,128)(2,1)} fusion(f32[8,6,197,197]{2,3,1,0:T(8,128)} %fusion.2, f32[8,6,197,197]{2,3,1,0:T(8,128)} %fusion.82, bf16[8,197,3,6,64]{1,4,3,2,0:T(8,128)(2,1)} %bitcast.97), kind=kOutput, calls=%fused_computation.101 | convolution fusion | flops 248371488 | bytes 42104832 | tf_op jit(solution)/shard_map/bhqk,bkhd->bqhd/dot_general | solution.py:125
  601.3 16.9 %fusion.73 = bf16[8,197,1,6,64]{1,4,3,0,2:T(8,128)(2,1)} fusion(f32[8,6,197,197]{2,3,1,0:T(8,128)} %fusion.2, f32[8,6,197,197]{2,3,1,0:T(8,128)} %fusion.82, bf16[8,197,3,6,64]{1,4,3,2,0:T(8,128)(2,1)} %bitcast.98), kind=kOutput, calls=%fused_computation.100 | convolution fusion | flops 248371488 | bytes 42104832 | tf_op jit(solution)/shard_map/bhqk,bqhd->bkhd/dot_general | solution.py:128
  618.2 2.5 pad_maximum_fusion
  621.4 12.9 %copy.102 = bf16[1,8,197,1152]{2,1,0,3:T(8,128)(2,1)} copy(bf16[1,8,197,1152]{2,3,1,0:T(8,128)(2,1)S(1)} %bitcast.99) | data formatting | bytes 7262208 | tf_op jit(solution)/shard_map/convert_element_type | solution.py:135
  634.3 5.0 all-to-all-start.2
  639.3 7.3 convolution_convert_fusion.5
  646.9 7.3 fusion.84
  654.4 5.1 convolution_convert_fusion.7
  659.5 33.6 %all-to-all-done.2 = bf16[1,8,197,1152]{2,1,0,3:T(8,128)(2,1)} async-done(((bf16[1,8,197,1152]{2,1,0,3:T(8,128)(2,1)}), bf16[1,8,197,1152]{2,1,0,3:T(8,128)(2,1)}, u32[]{:S(2)}, u32[]{:S(2)}) %all-to-all-start.2) | async-done | bytes 3631136 | tf_op jit(solution)/shard_map/all_to_all | solution.py:214
  693.1 12.9 %copy.110 = bf16[1,8,197,4,288]{4,3,1,2,0:T(4,128)(2,1)} copy(bf16[1,8,197,4,288]{2,1,4,3,0:T(8,128)(2,1)} %bitcast.20) | data formatting | bytes 7262208 | tf_op jit(solution)/shard_map/all_to_all | solution.py:214
  706.0 14.4 %copy.104 = bf16[4,1,8,197,288]{3,2,0,4,1:T(8,128)(2,1)} copy(bf16[4,1,8,197,288]{4,0,2,3,1:T(4,128)(2,1)} %bitcast.93) | data formatting | bytes 7262208 | tf_op jit(solution)/shard_map/all_to_all | solution.py:214
  720.4 9.2 reshape.118
  729.6 7.0 convolution_convert_fusion.6
  736.9 7.5 convolution_convert_fusion
  745.9 23.6 %reduce-scatter.24.cloned.1.call-done = bf16[48,384]{1,0:T(8,128)(2,1)} async-done(((bf16[384,384]{1,0:T(8,128)(2,1)}), bf16[48,384]{1,0:T(8,128)(2,1)}) %reduce-scatter.24.cloned.1.call-update) | async-done | bytes 36880 | tf_op jit(solution)/shard_map/reduce_scatter | solution.py:242
  771.0 59.5 %reduce-scatter.22.cloned.1.call-done = bf16[96,48]{0,1:T(8,128)(2,1)} async-done(((bf16[96,384]{0,1:T(8,128)(2,1)}), bf16[96,48]{0,1:T(8,128)(2,1)}) %reduce-scatter.22.cloned.1.call-update) | async-done | bytes 9232 | tf_op jit(solution)/shard_map/reduce_scatter | solution.py:239
  831.8 4.6 convert_reduce_fusion
  836.4 55.9 %reduce-scatter.20.cloned.1.call-done = bf16[48,288]{1,0:T(8,128)(2,1)} async-done(((bf16[384,288]{1,0:T(8,128)(2,1)}), bf16[48,288]{1,0:T(8,128)(2,1)}) %reduce-scatter.20.cloned.1.call-update) | async-done | bytes 27664 | tf_op jit(solution)/shard_map/reduce_scatter | solution.py:236
  893.7 49.2 %reduce-scatter.36.cloned.1.call-done = bf16[1576,384]{1,0:T(8,128)(2,1)} async-done(((bf16[6304,384]{1,0:T(8,128)(2,1)}), bf16[1576,384]{1,0:T(8,128)(2,1)}) %reduce-scatter.36.cloned.1.call-update) | async-done | bytes 1210384
  942.9 2.7 fusion.50
  946.5 3.7 fusion.44
  950.2 16.2 %reduce-scatter.28.cloned.1.call-done = f32[96,6]{1,0:T(8,128)} async-done(((f32[384,6]{1,0:T(8,128)}), f32[96,6]{1,0:T(8,128)}) %reduce-scatter.28.cloned.1.call-update) | async-done | bytes 2320
  968.1 22.2 %all-reduce.4 = (f32[288]{0:T(512)}, f32[96]{0:T(128)}, f32[384]{0:T(512)}, f32[96]{0:T(128)}, f32[96]{0:T(128)}, /*index=5*/f32[96]{0:T(128)}, f32[96]{0:T(128)}, f32[96]{0:T(128)}) all-reduce(f32[288]{0:T(512)S(1)} %convert_reduce_fusion, f32[96]{0:T(128)S(1)} %bitcast.113, ...), channel_id=1, replica_groups=mesh['dp'=8,'col'=4] {'dp'}, use_global_device_ids=true, to_apply=%region_19.20 | all-reduce | flops 1248 | bytes 9984 | tf_op jit(solution)/shard_map/psum | solution.py:249
  (118 shorter events, 25.9 us)
Async XLA Ops:
  7.2 4.9 copy-start.16
  7.2 45.8 %copy-start.25 = (f32[288]{0:T(512)S(1)}, f32[288]{0:T(512)}, u32[]{:S(2)}) copy-start(f32[288]{0:T(512)} %param.16) | copy-start | bytes 3460
  7.2 45.8 %all-gather.5.cloned.1.call-start = ((), (), s32[]{:S(2)}) async-start(), calls=%async_computation.12 | async-start | bytes 6051840 | tf_op jit(solution)/shard_map/all_gather | solution.py:64
  9.1 3.0 copy-start.12
  9.1 3.0 copy-start.14
  44.7 14.6 %copy-start.10 = (bf16[384,288]{1,0:T(8,128)(2,1)}, bf16[384,288]{1,0:T(8,128)(2,1)S(1)}, u32[]{:S(2)}) copy-start(bf16[384,288]{1,0:T(8,128)(2,1)S(1)} %all_gather.25) | copy-start | bytes 663556
  80.3 2.1 copy-start.2
  84.3 27.8 %collective-permute-start = (bf16[1,1,8,197,288]{3,4,0,2,1:T(8,128)(2,1)}, bf16[1,1,8,197,288]{3,4,0,2,1:T(8,128)(2,1)}, u32[]{:S(2)}, u32[]{:S(2)}) collective-permute-start(bf16[1,1,8,197,288]{3,4,0,2,1:T(8,128)(2,1)} %get-tuple-element.38), channel_id=1, source_target_pairs={{0,1},{1,2},{2,3},{3,0},{4,5},{5,6},{6,7},{7,4},{8,9},{9,10},{10,1... | collective-permute-start | bytes 2723336 | tf_op jit(solution)/shard_map/ppermute | solution.py:37
  84.5 30.0 %collective-permute-start.1 = (bf16[1,1,8,197,288]{3,4,0,2,1:T(8,128)(2,1)}, bf16[1,1,8,197,288]{3,4,0,2,1:T(8,128)(2,1)S(1)}, u32[]{:S(2)}, u32[]{:S(2)}) collective-permute-start(bf16[1,1,8,197,288]{3,4,0,2,1:T(8,128)(2,1)} %get-tuple-element.37), channel_id=1, source_target_pairs={{0,2},{1,3},{2,0},{3,1},{4,6},{5,7},{6,4},{7,5},{8,10},{9,11},{10,... | collective-permute-start | bytes 2723336 | tf_op jit(solution)/shard_map/ppermute | solution.py:37
  84.8 51.1 %collective-permute-start.2 = (bf16[1,1,8,197,288]{3,4,0,2,1:T(8,128)(2,1)}, bf16[1,1,8,197,288]{3,4,0,2,1:T(8,128)(2,1)S(1)}, u32[]{:S(2)}, u32[]{:S(2)}) collective-permute-start(bf16[1,1,8,197,288]{3,4,0,2,1:T(8,128)(2,1)} %get-tuple-element.36), channel_id=1, source_target_pairs={{0,3},{1,0},{2,1},{3,2},{4,7},{5,4},{6,5},{7,6},{8,11},{9,8},{10,9... | collective-permute-start | bytes 2723336 | tf_op jit(solution)/shard_map/ppermute | solution.py:37
  154.8 5.7 copy-start.22
  156.9 34.8 %all-to-all-start = ((bf16[1,8,197,384]{2,1,0,3:T(8,128)(2,1)}), bf16[1,8,197,384]{2,1,0,3:T(8,128)(2,1)S(1)}, u32[]{:S(2)}, u32[]{:S(2)}) async-start(bf16[1,8,197,384]{2,1,0,3:T(8,128)(2,1)} %copy.93), calls=%async_computation | async-start | bytes 3145728 | tf_op jit(solution)/shard_map/all_to_all | solution.py:173
  160.4 100.6 %reduce-scatter.30.cloned.1.call-start = ((), (), s32[]{:S(2)}) async-start(), calls=%async_computation.21 | async-start | bytes 6051840
  191.6 1.1 copy-start.7
  206.7 3.8 copy-start.5
  210.5 50.6 %copy-start = (bf16[1576,384]{1,0:T(8,128)(2,1)S(1)}, bf16[1576,384]{1,0:T(8,128)(2,1)}, u32[]{:S(2)}) copy-start(bf16[1576,384]{1,0:T(8,128)(2,1)} %param.14) | copy-start | bytes 3631108
  210.5 50.6 %copy-start.19 = (f32[384]{0:T(512)S(1)}, f32[384]{0:T(512)}, u32[]{:S(2)}) copy-start(f32[384]{0:T(512)} %param.18) | copy-start | bytes 4612
  210.5 52.6 %copy-start.20 = (f32[384]{0:T(512)S(1)}, f32[384]{0:T(512)}, u32[]{:S(2)}) copy-start(f32[384]{0:T(512)} %param.25) | copy-start | bytes 4612
  210.5 52.6 %copy-start.23 = (f32[384]{0:T(512)S(1)}, f32[384]{0:T(512)}, u32[]{:S(2)}) copy-start(f32[384]{0:T(512)} %param.26) | copy-start | bytes 4612
  210.5 56.2 %copy-start.17 = (bf16[48,384]{1,0:T(8,128)(2,1)S(1)}, bf16[48,384]{1,0:T(8,128)(2,1)}, u32[]{:S(2)}) copy-start(bf16[48,384]{1,0:T(8,128)(2,1)} %param.19) | copy-start | bytes 110596
  210.5 87.2 %copy-start.18 = (bf16[384,48]{0,1:T(8,128)(2,1)S(1)}, bf16[384,48]{0,1:T(8,128)(2,1)}, u32[]{:S(2)}) copy-start(bf16[384,48]{0,1:T(8,128)(2,1)} %param.21) | copy-start | bytes 110596
  210.5 129.0 %copy-start.26 = (f32[384]{0:T(512)S(1)}, f32[384]{0:T(512)}, u32[]{:S(2)}) copy-start(f32[384]{0:T(512)} %param.20) | copy-start | bytes 4612
  210.6 129.0 %all-gather.7.cloned.1.call-start = ((), (), s32[]{:S(2)}) async-start(), calls=%async_computation.13 | async-start | bytes 6051840 | tf_op jit(solution)/shard_map/all_gather | solution.py:64
  266.1 99.9 %all-gather.9.cloned.1.call-start = ((), (), s32[]{:S(2)}) async-start(), calls=%async_computation.14 | async-start | bytes 6051840 | tf_op jit(solution)/shard_map/all_gather | solution.py:64
  266.7 165.2 %reduce-scatter.34.cloned.1.call-start = ((), (), s32[]{:S(2)}) async-start(), calls=%async_computation.23 | async-start | bytes 6051840
  375.2 2.2 copy-start.1
  382.6 100.8 %reduce-scatter.32.cloned.1.call-start = ((), (), s32[]{:S(2)}) async-start(), calls=%async_computation.22 | async-start | bytes 6051840
  390.3 41.6 %copy-start.4 = (bf16[1576,384]{1,0:T(8,128)(2,1)S(1)}, bf16[1576,384]{1,0:T(8,128)(2,1)}, u32[]{:S(2)}) copy-start(bf16[1576,384]{1,0:T(8,128)(2,1)} %reduce-scatter.30.cloned.1.call-done) | copy-start | bytes 3631108
  390.3 93.1 %copy-start.24 = (f32[384]{0:T(512)S(1)}, f32[384]{0:T(512)}, u32[]{:S(2)}) copy-start(f32[384]{0:T(512)} %param.22) | copy-start | bytes 4612
  390.3 138.7 %all-gather.11.cloned.1.call-start = ((), (), s32[]{:S(2)}) async-start(), calls=%async_computation.15 | async-start | bytes 6051840 | tf_op jit(solution)/shard_map/all_gather | solution.py:64
  488.0 1.4 copy-start.3
  541.3 23.6 %all-to-all-start.1 = ((bf16[4,8,197,96]{2,1,3,0:T(8,128)(2,1)}), bf16[4,8,197,96]{2,1,3,0:T(8,128)(2,1)S(1)}, u32[]{:S(2)}, u32[]{:S(2)}) async-start(bf16[4,8,197,96]{2,1,3,0:T(8,128)(2,1)} %copy.96), calls=%async_computation.1 | async-start | bytes 3145728 | tf_op jit(solution)/shard_map/all_to_all | solution.py:210
  566.4 11.7 %copy-start.8 = (bf16[1,8,197,4,96]{2,4,3,1,0:T(8,128)(2,1)S(1)}, bf16[1,8,197,4,96]{2,4,3,1,0:T(8,128)(2,1)}, u32[]{:S(2)}) copy-start(bf16[1,8,197,4,96]{2,4,3,1,0:T(8,128)(2,1)} %copy.97) | copy-start | bytes 3631108
  601.3 16.9 %copy-start.9 = (bf16[8,197,1,6,64]{1,4,3,0,2:T(8,128)(2,1)S(1)}, bf16[8,197,1,6,64]{1,4,3,0,2:T(8,128)(2,1)}, u32[]{:S(2)}) copy-start(bf16[8,197,1,6,64]{1,4,3,0,2:T(8,128)(2,1)} %fusion.79) | copy-start | bytes 3631108
  634.3 58.8 %all-to-all-start.2 = ((bf16[1,8,197,1152]{2,1,0,3:T(8,128)(2,1)}), bf16[1,8,197,1152]{2,1,0,3:T(8,128)(2,1)}, u32[]{:S(2)}, u32[]{:S(2)}) async-start(bf16[1,8,197,1152]{2,1,0,3:T(8,128)(2,1)} %copy.102), calls=%async_computation.2 | async-start | bytes 9437184 | tf_op jit(solution)/shard_map/all_to_all | solution.py:214
  639.3 105.2 %reduce-scatter.26.cloned.1.call-start = ((), (), s32[]{:S(2)}) async-start(), calls=%async_computation.19 | async-start | bytes 331776 | tf_op jit(solution)/shard_map/reduce_scatter | solution.py:245
  646.7 7.7 copy-start.6
  646.7 122.9 %reduce-scatter.24.cloned.1.call-start = ((), (), s32[]{:S(2)}) async-start(), calls=%async_computation.18 | async-start | bytes 331776 | tf_op jit(solution)/shard_map/reduce_scatter | solution.py:242
  654.3 176.1 %reduce-scatter.22.cloned.1.call-start = ((), (), s32[]{:S(2)}) async-start(), calls=%async_computation.17 | async-start | bytes 110592 | tf_op jit(solution)/shard_map/reduce_scatter | solution.py:239
  659.5 232.8 %reduce-scatter.20.cloned.1.call-start = ((), (), s32[]{:S(2)}) async-start(), calls=%async_computation.16 | async-start | bytes 331776 | tf_op jit(solution)/shard_map/reduce_scatter | solution.py:236
  729.6 7.4 copy-start.11
  736.6 206.3 %reduce-scatter.36.cloned.1.call-start = ((), (), s32[]{:S(2)}) async-start(), calls=%async_computation.24 | async-start | bytes 6051840
  744.4 198.5 %copy-start.13 = (f32[1576]{0:T(1024)S(1)}, f32[1576]{0:T(1024)}, u32[]{:S(2)}) copy-start(f32[1576]{0:T(1024)} %copy-done.12) | copy-start | bytes 18916
  744.4 198.5 %copy-start.15 = (f32[1576]{0:T(1024)S(1)}, f32[1576]{0:T(1024)}, u32[]{:S(2)}) copy-start(f32[1576]{0:T(1024)} %copy-done.14) | copy-start | bytes 18916
  744.4 198.5 %copy-start.21 = (f32[384]{0:T(512)S(1)}, f32[384]{0:T(512)}, u32[]{:S(2)}) copy-start(f32[384]{0:T(512)} %param.23) | copy-start | bytes 4612
  744.5 222.0 %reduce-scatter.28.cloned.1.call-start = ((), (), s32[]{:S(2)}) async-start(), calls=%async_computation.20 | async-start | bytes 245760
Sparse Core Ops, SparseCore 0:
  12.1 40.8 all-gather.4
  210.6 50.3 reduce-scatter.29
  266.2 38.1 all-gather.6
  305.8 38.1 all-gather.8
  382.7 49.1 reduce-scatter.33
  434.3 49.0 reduce-scatter.31
  490.8 38.1 all-gather.10
  646.8 60.8 reduce-scatter.25
  711.0 58.5 reduce-scatter.23
  772.7 57.7 reduce-scatter.21
  833.7 58.5 reduce-scatter.19
  894.7 48.1 reduce-scatter.35
  946.6 19.7 reduce-scatter.27
